TPU v7x, 32 devices: a whole 2x2x4 slice. The times are simulated.
32 devices in a mesh: row: 8 (over z, x), col: 4 (over y, core).
Axes of the slice: x: 2, y: 2, z: 4, core: 2. Of those that a mesh axis runs over, the one named last changes fastest.
Arguments:
- normal_matrix: float32 [9216, 9216], P('row', 'col'), may hold values from -1 to 6, as said below
- right_side: float32 [9216, 64], P('col'), may hold values from -6 to 6
- tile_inverse: float32 [72, 128, 128], P('col'), may hold values from -1 to 3.5, as said below
- order_ids: int32 [9216], P('col'), may hold values from 0 to 96, never falling along the last dimension, each value on 1 to 194 neighbouring positions
Outputs:
- solution: float32 [9216, 64], P('col')
- residual: float32 [9216, 64], P('col')
Inputs may be any that keep to these rules, and one draw needn't show every extreme that they name: `normal_matrix`: symmetric and positive definite. `tile_inverse`: each tile symmetric, every principal submatrix of it positive definite. `order_ids`: never falling along the coefficients; each order holds 1 to 194 coefficients.
All inputs are finite; a program needn't handle non-finite values.
Results may differ from a plain program's by a relative error of at most 0.0003.
Values sent between devices are 32-bit elements; how exact they have to be, the bound alone decides.
A program may use at most 64 MiB of HBM per device.

v0:
```python
import jax
import jax.numpy as jnp
from jax import lax
from jax.sharding import PartitionSpec as P

ITERS = 2


def apply_precond(tile_inverse, order_ids, vector):
    count = tile_inverse.shape[0]
    width = tile_inverse.shape[1]
    order_tile = order_ids.reshape(count, width)
    same_order = order_tile[:, :, None] == order_tile[:, None, :]
    masked = jnp.where(same_order, tile_inverse, jnp.float32(0.0))
    pieces = vector.reshape(count, width, vector.shape[1])
    result = jnp.einsum("tij,tjk->tik", masked, pieces, precision=lax.Precision.HIGHEST)
    return result.reshape(vector.shape)


def body(normal_matrix, right_side, tile_inverse, order_ids):
    block_rows = normal_matrix.shape[0]

    def apply_matrix(vector):
        first_row = lax.axis_index("row") * block_rows
        gathered = lax.all_gather(vector, "col", axis=0, tiled=True)
        row_piece = lax.dynamic_slice_in_dim(gathered, first_row, block_rows, 0)
        partial_value = lax.dot_general(
            normal_matrix,
            row_piece,
            (((0,), (0,)), ((), ())),
            precision=lax.Precision.HIGHEST,
            preferred_element_type=jnp.float32,
        )
        return lax.psum(partial_value, "row")

    solution = jnp.zeros_like(right_side)
    residual = right_side
    precond_res = apply_precond(tile_inverse, order_ids, residual)
    image_res = apply_matrix(precond_res)
    image_dir = jnp.zeros_like(right_side)
    precond_dir = jnp.zeros_like(right_side)
    residual_dir = jnp.zeros_like(right_side)
    direction = jnp.zeros_like(right_side)
    gamma_prev = jnp.ones((right_side.shape[1],), jnp.float32)
    alpha_prev = jnp.ones((right_side.shape[1],), jnp.float32)
    for iteration in range(ITERS):
        gamma_now, delta_now = lax.psum(
            (jnp.sum(residual * precond_res, axis=0), jnp.sum(image_res * precond_res, axis=0)),
            "col",
        )
        precond_img = apply_precond(tile_inverse, order_ids, image_res)
        image_img = apply_matrix(precond_img)
        if iteration == 0:
            beta_ratio = jnp.zeros_like(gamma_now)
            step_size = gamma_now / delta_now
        else:
            beta_ratio = gamma_now / gamma_prev
            step_size = gamma_now / (delta_now - beta_ratio * gamma_now / alpha_prev)
        image_dir = image_img + beta_ratio * image_dir
        precond_dir = precond_img + beta_ratio * precond_dir
        residual_dir = image_res + beta_ratio * residual_dir
        direction = precond_res + beta_ratio * direction
        solution = solution + step_size * direction
        residual = residual - step_size * residual_dir
        precond_res = precond_res - step_size * precond_dir
        image_res = image_res - step_size * image_dir
        gamma_prev = gamma_now
        alpha_prev = step_size
    return (solution, residual)


def solution(mesh):
    return jax.shard_map(
        body,
        mesh=mesh,
        in_specs=(P("row", "col"), P("col", None), P("col", None, None), P("col")),
        out_specs=(P("col", None), P("col", None)),
        check_vma=False,
    )
```

profile of v0, /device:TPU:0, one launch (start us, length us, event | category | flops | bytes accessed | tf_op | source)
XLA Modules:
  0.0 251.0 jit_solution(8097218119773810578)
XLA Ops:
  7.2 0.0 all-gather.3.cloned.1.call-start
  7.2 3.9 %convolution_bitcast_fusion.3 = f32[18,8,8,128]{3,2,1,0:T(8,128)S(1)} fusion(f32[18,128,128]{2,1,0:T(8,128)} %param.6, s32[18,128]{1,0:T(8,128)} %bitcast.55, f32[2304,64]{0,1:T(8,128)} %param.5), kind=kOutput, calls=%fused_computation.3 | convolution fusion | flops 227082240 | bytes 2368512 | tf_op jit(solution)/shard_map/tij,tjk->tik/dot_general | solution.py:16
  11.1 0.9 copy.50
  11.9 0.0 all-gather.3.cloned.1.call-update
  12.0 0.0 all-reduce.5.cloned.1.call-start
  12.0 0.0 copy-start.4
  12.0 26.9 %all-gather.3.cloned.1.call-done = f32[9216,64]{0,1:T(8,128)} async-done(((f32[2304,64]{0,1:T(8,128)}), f32[9216,64]{0,1:T(8,128)}) %all-gather.3.cloned.1.call-update) | async-done | bytes 2359312 | tf_op jit(solution)/shard_map/all_gather | solution.py:25
  38.9 0.0 copy-start.2
  38.9 11.4 %convolution_bitcast_fusion.1 = f32[2304,64]{0,1:T(8,128)} fusion(f32[1152,2304]{1,0:T(8,128)} %param.4, f32[9216,64]{0,1:T(8,128)} %all-gather.3.cloned.1.call-done, s32[]{:T(128)S(6)} %select_n.10), kind=kOutput, calls=%fused_computation.1 | convolution fusion | flops 2038431744 | bytes 11501572 | tf_op jit(solution)/shard_map/dot_general | solution.py:27
  50.3 0.0 all-reduce.5.cloned.1.call-update
  50.3 0.0 all-gather.5.cloned.1.call-start
  50.3 73.3 %all-reduce.5.cloned.1.call-done = f32[2304,64]{0,1:T(8,128)} async-done(((f32[2304,64]{0,1:T(8,128)}), f32[2304,64]{0,1:T(8,128)}) %all-reduce.5.cloned.1.call-update) | async-done | bytes 589840 | tf_op jit(solution)/shard_map/psum | solution.py:34
  123.7 0.0 copy-done.4
  123.7 0.0 copy-done.2
  123.7 3.5 %convolution_bitcast_fusion.2 = f32[18,8,8,128]{3,2,1,0:T(8,128)S(1)} fusion(f32[18,128,128]{2,1,0:T(8,128)S(1)} %copy-done.2, s32[18,128]{1,0:T(8,128)S(1)} %bitcast.56, f32[2304,64]{0,1:T(8,128)} %all-reduce.5.cloned.1.call-done), kind=kOutput, calls=%fused_computation.2 | convolution fusion | flops 227082240 | bytes 2368512 | tf_op jit(solution)/shard_map/tij,tjk->tik/dot_general | solution.py:16
  127.2 0.9 copy.49
  128.0 0.0 all-gather.5.cloned.1.call-update
  128.1 0.0 copy-start
  128.1 0.0 copy-start.1
  128.1 0.2 all-reduce.7.cloned.1.call-start
  128.3 22.9 %all-gather.5.cloned.1.call-done = f32[9216,64]{0,1:T(8,128)} async-done(((f32[2304,64]{0,1:T(8,128)}), f32[9216,64]{0,1:T(8,128)}) %all-gather.5.cloned.1.call-update) | async-done | bytes 2359312 | tf_op jit(solution)/shard_map/all_gather | solution.py:25
  151.2 11.3 %convolution_bitcast_fusion = f32[2304,64]{0,1:T(8,128)} fusion(f32[1152,2304]{1,0:T(8,128)} %param.4, f32[9216,64]{0,1:T(8,128)} %all-gather.5.cloned.1.call-done, s32[]{:T(128)S(6)} %select_n.10), kind=kOutput, calls=%fused_computation | convolution fusion | flops 2038431744 | bytes 11501572 | tf_op jit(solution)/shard_map/dot_general | solution.py:27
  162.5 0.0 all-reduce.7.cloned.1.call-update
  162.5 0.0 copy-done
  162.6 0.0 copy-done.1
  162.6 0.2 multiply_reduce_fusion.2
  162.8 5.9 %all-reduce.1 = (f32[64]{0:T(128)S(1)}, f32[64]{0:T(128)S(1)}) all-reduce(f32[64]{0:T(128)S(1)} %get-tuple-element.5, f32[64]{0:T(128)S(1)} %get-tuple-element.4), channel_id=1, replica_groups=mesh['row'=8,'col'=4] {'col'}, use_global_device_ids=true, to_apply=%region_1.2 | all-reduce | flops 128 | bytes 1024 | tf_op jit(solution)/shard_map/psum | solution.py:47
  168.7 67.3 %all-reduce.7.cloned.1.call-done = f32[2304,64]{0,1:T(8,128)} async-done(((f32[2304,64]{0,1:T(8,128)}), f32[2304,64]{0,1:T(8,128)}) %all-reduce.7.cloned.1.call-update) | async-done | bytes 589840 | tf_op jit(solution)/shard_map/psum | solution.py:34
  235.9 0.0 copy-start.3
  235.9 1.5 multiply_reduce_fusion
  237.4 5.7 %all-reduce = (f32[64]{0:T(128)S(1)}, f32[64]{0:T(128)S(1)}) all-reduce(f32[64]{0:T(128)S(1)} %get-tuple-element.3, f32[64]{0:T(128)S(1)} %get-tuple-element.2), channel_id=1, replica_groups=mesh['row'=8,'col'=4] {'col'}, use_global_device_ids=true, to_apply=%region_6.7 | all-reduce | flops 128 | bytes 1024 | tf_op jit(solution)/shard_map/psum | solution.py:47
  243.1 0.0 copy-done.3
  243.1 1.4 multiply_subtract_fusion
  (2 shorter events, 0.0 us)
Async XLA Ops:
  7.2 31.7 %all-gather.3.cloned.1.call-start = ((), (), s32[]{:S(2)}) async-start(), calls=%async_computation | async-start | bytes 2949120 | tf_op jit(solution)/shard_map/all_gather | solution.py:25
  12.0 111.7 %all-reduce.5.cloned.1.call-start = ((), (), s32[]{:S(2)}) async-start(), calls=%async_computation.1 | async-start | bytes 1179648 | tf_op jit(solution)/shard_map/psum | solution.py:34
  12.0 111.7 %copy-start.4 = (s32[2304]{0:T(1024)S(1)}, s32[2304]{0:T(1024)}, u32[]{:S(2)}) copy-start(s32[2304]{0:T(1024)} %param.7) | copy-start | bytes 27652
  38.9 84.8 %copy-start.2 = (f32[18,128,128]{2,1,0:T(8,128)S(1)}, f32[18,128,128]{2,1,0:T(8,128)}, u32[]{:S(2)}) copy-start(f32[18,128,128]{2,1,0:T(8,128)} %param.6) | copy-start | bytes 3538948
  50.3 100.9 %all-gather.5.cloned.1.call-start = ((), (), s32[]{:S(2)}) async-start(), calls=%async_computation.2 | async-start | bytes 2949120 | tf_op jit(solution)/shard_map/all_gather | solution.py:25
  128.1 34.5 %copy-start = (f32[2304,64]{0,1:T(8,128)S(1)}, f32[2304,64]{0,1:T(8,128)}, u32[]{:S(2)}) copy-start(f32[2304,64]{0,1:T(8,128)} %param.5) | copy-start | bytes 1769476
  128.1 34.5 %copy-start.1 = (f32[2304,64]{0,1:T(8,128)S(1)}, f32[2304,64]{0,1:T(8,128)}, u32[]{:S(2)}) copy-start(f32[2304,64]{0,1:T(8,128)} %all-reduce.5.cloned.1.call-done) | copy-start | bytes 1769476
  128.1 107.9 %all-reduce.7.cloned.1.call-start = ((), (), s32[]{:S(2)}) async-start(), calls=%async_computation.3 | async-start | bytes 1179648 | tf_op jit(solution)/shard_map/psum | solution.py:34
  235.9 7.2 %copy-start.3 = (f32[2304,64]{0,1:T(8,128)S(1)}, f32[2304,64]{0,1:T(8,128)}, u32[]{:S(2)}) copy-start(f32[2304,64]{0,1:T(8,128)} %all-reduce.7.cloned.1.call-done) | copy-start | bytes 1769476
Sparse Core Ops, SparseCore 0:
  12.1 26.7 all-gather.2
  50.4 73.2 all-reduce.4
  128.2 22.9 all-gather.4
  162.7 73.2 all-reduce.6
where the time goes:
time: 251 us
  waiting for transfers between devices  190 us (76%)
  matrix products  30 us (12%)
  between operations  13.8 us (5%)
  blocking collectives  11.5 us (5%)
  other arithmetic  3.1 us (1%)
    psum x2, waiting for transfers between devices, apply_matrix(): return lax.psum(partial_value, 'row')  141 us
    all_gather x2, waiting for transfers between devices, apply_matrix(): gathered = lax.all_gather(vector, 'col', axis=0, tiled=True)  49.8 us
    dot_general x2, matrix products, apply_matrix(): lax.dot_general(normal_matrix, row_piece, (((0,), (0,)), ((), ())), preci...  22.7 us
    psum x2, blocking collectives, body(): lax.psum((jnp.sum(residual * precond_res, axis=0), jnp.sum(image_res * pr...  11.5 us
    dot_general x2, matrix products, apply_precond(): jnp.einsum('tij,tjk->tik', masked, pieces, precision=lax.Precision.HIGHEST)  7.35 us
  transfers between devices with their start and end apart: 4, of which 4 were waited for; matrix products, arithmetic and copies ran while one was open for 0% of the time, Pallas kernels for 0%

commit v1 on v0

--- a/solution.py
+++ b/solution.py
@@ -1,23 +1,34 @@
+import functools
+
 import jax
 import jax.numpy as jnp
 from jax import lax
+from jax.experimental import pallas as pl
+from jax.experimental.pallas import tpu as pltpu
 from jax.sharding import PartitionSpec as P
 
 ITERS = 2
-
-
-def apply_precond(tile_inverse, order_ids, vector):
+MESH = pl.DeviceIdType.MESH
+
+
+def masked_tiles(tile_inverse, order_ids):
     count = tile_inverse.shape[0]
     width = tile_inverse.shape[1]
     order_tile = order_ids.reshape(count, width)
     same_order = order_tile[:, :, None] == order_tile[:, None, :]
-    masked = jnp.where(same_order, tile_inverse, jnp.float32(0.0))
+    return jnp.where(same_order, tile_inverse, jnp.float32(0.0))
+
+
+def apply_precond(tile_inverse, order_ids, vector):
+    count = tile_inverse.shape[0]
+    width = tile_inverse.shape[1]
+    masked = masked_tiles(tile_inverse, order_ids)
     pieces = vector.reshape(count, width, vector.shape[1])
     result = jnp.einsum("tij,tjk->tik", masked, pieces, precision=lax.Precision.HIGHEST)
     return result.reshape(vector.shape)
 
 
-def body(normal_matrix, right_side, tile_inverse, order_ids):
+def plain_body(normal_matrix, right_side, tile_inverse, order_ids):
     block_rows = normal_matrix.shape[0]
 
     def apply_matrix(vector):
@@ -69,9 +80,332 @@
     return (solution, residual)
 
 
+def split(value):
+    high = value.astype(jnp.bfloat16)
+    low = (value - high.astype(jnp.float32)).astype(jnp.bfloat16)
+    return jnp.concatenate([high, low], axis=0)
+
+
+def times_transposed(left, right):
+    return lax.dot_general(
+        left, right, (((1,), (1,)), ((), ())), preferred_element_type=jnp.float32
+    )
+
+
+def fold(product, rows, columns):
+    upper = product[:rows, :columns] + product[rows:, :columns]
+    lower = product[:rows, columns:] + product[rows:, columns:]
+    return upper + lower
+
+
+def kernel(
+    row_count, group, chunks, width,
+    a_ref, tile_ref, b_ref,
+    sol_ref, res_ref,
+    a_buf, a_split, tile_split, v_split, u_buf, m_buf,
+    part, near, half, far, full, image,
+    dot_own, dot_in,
+    a_sem, near_sem, far_sem, full_sem, line_recv, line_send, side_recv, side_send, dot_send, dot_recv,
+):
+    my_row, my_col = lax.axis_index("row"), lax.axis_index("col")
+    depth = row_count // group
+    place, lane = my_row // group, lax.rem(my_row, group)
+    core = lax.rem(my_col, 2)
+    partner = my_col + 1 - 2 * core
+    across = lax.rem(my_col + 2, 4)
+    nrhs, block_cols = b_ref.shape
+    block_rows = a_ref.shape[0]
+    hh = nrhs // 2
+    tiles = block_cols // width
+    steps = block_rows // width
+    piece = block_rows // chunks
+
+    def fetch(i):
+        rows = pl.ds(pl.multiple_of(i * width, width), width)
+        return pltpu.make_async_copy(a_ref.at[rows], a_buf.at[i], a_sem.at[i])
+
+    @pl.loop(0, steps)
+    def _(i):
+        fetch(i).start()
+
+    barrier = pltpu.get_barrier_semaphore()
+    for shift in range(1, 4):
+        pl.semaphore_signal(
+            barrier, inc=1, device_id=(my_row, lax.rem(my_col + shift, 4)), device_id_type=MESH
+        )
+    for shift in range(1, group):
+        side = place * group + lax.rem(lane + shift, group)
+        pl.semaphore_signal(barrier, inc=1, device_id=(side, my_col), device_id_type=MESH)
+
+    @pl.when(place > 0)
+    def _():
+        pl.semaphore_signal(barrier, inc=1, device_id=(my_row - group, my_col), device_id_type=MESH)
+
+    @pl.when(place < depth - 1)
+    def _():
+        pl.semaphore_signal(barrier, inc=1, device_id=(my_row + group, my_col), device_id_type=MESH)
+
+    def tile_lanes(t):
+        return pl.ds(pl.multiple_of(t * width, width), width)
+
+    def precondition(source, target):
+        @pl.loop(0, tiles)
+        def _(t):
+            lanes = tile_lanes(t)
+            value = fold(times_transposed(split(source[:, lanes]), tile_split[t]), nrhs, width)
+            target[:, lanes] = value
+            v_split[:, lanes] = split(value)
+
+    @pl.loop(0, tiles)
+    def _(t):
+        tile_split[t] = split(tile_ref[t])
+
+    precondition(b_ref, u_buf)
+
+    def reduce_and_spread(turn):
+        def swap(source, target, sem, column):
+            return pltpu.make_async_remote_copy(
+                src_ref=source, dst_ref=target, send_sem=sem.at[turn, 0], recv_sem=sem.at[turn, 1],
+                device_id=(my_row, column), device_id_type=MESH,
+            )
+
+        mine = pl.ds(pl.multiple_of(core * hh, hh), hh)
+        other = pl.ds(pl.multiple_of((1 - core) * hh, hh), hh)
+        first = swap(part.at[turn, other], near.at[turn], near_sem, partner)
+        first.start()
+        first.wait()
+        half[turn] = part[turn, mine] + near[turn]
+        second = swap(half.at[turn], far.at[turn], far_sem, across)
+        second.start()
+        second.wait()
+        full[turn, mine] = half[turn] + far[turn]
+        third = swap(full.at[turn, mine], full.at[turn, mine], full_sem, partner)
+        third.start()
+        third.wait()
+
+        @pl.when(place == my_col)
+        def _():
+            start = pl.multiple_of(lane * block_rows, width)
+            image[turn, :, pl.ds(start, block_rows)] = full[turn]
+
+        def lanes_of(owner, q):
+            start = pl.multiple_of(owner * block_rows + q * piece, width)
+            return image.at[turn, :, pl.ds(start, piece)]
+
+        def along(q, way, target_row):
+            return pltpu.make_async_remote_copy(
+                src_ref=lanes_of(lane, q), dst_ref=lanes_of(lane, q),
+                send_sem=line_send.at[turn, way, q], recv_sem=line_recv.at[turn, q],
+                device_id=(target_row, my_col), device_id_type=MESH,
+            )
+
+        def sideways(q, shift):
+            side = place * group + lax.rem(lane + shift, group)
+            return pltpu.make_async_remote_copy(
+                src_ref=lanes_of(lane, q), dst_ref=lanes_of(lane, q),
+                send_sem=side_send.at[turn, shift - 1, q], recv_sem=side_recv.at[turn, shift - 1, q],
+                device_id=(side, my_col), device_id_type=MESH,
+            )
+
+        def arrived(q, shift):
+            origin = lax.rem(lane + group - shift, group)
+            return pltpu.make_async_remote_copy(
+                src_ref=lanes_of(origin, q), dst_ref=lanes_of(origin, q),
+                send_sem=side_send.at[turn, shift - 1, q], recv_sem=side_recv.at[turn, shift - 1, q],
+                device_id=(place * group + origin, my_col), device_id_type=MESH,
+            )
+
+        goes_up = jnp.logical_and(place >= my_col, place < depth - 1)
+        goes_down = jnp.logical_and(place <= my_col, place > 0)
+        for q in range(chunks):
+            @pl.when(place != my_col)
+            def _():
+                along(q, 0, my_row).wait_recv()
+
+            @pl.when(goes_up)
+            def _():
+                along(q, 0, my_row + group).start()
+
+            @pl.when(goes_down)
+            def _():
+                along(q, 1, my_row - group).start()
+
+            for shift in range(1, group):
+                sideways(q, shift).start()
+
+        for q in range(chunks):
+            for shift in range(1, group):
+                arrived(q, shift).wait_recv()
+
+        def finish():
+            for q in range(chunks):
+                @pl.when(goes_up)
+                def _():
+                    along(q, 0, my_row + group).wait_send()
+
+                @pl.when(goes_down)
+                def _():
+                    along(q, 1, my_row - group).wait_send()
+
+                for shift in range(1, group):
+                    sideways(q, shift).wait_send()
+
+        return finish
+
+    def dots_copy(turn, shift):
+        return pltpu.make_async_remote_copy(
+            src_ref=dot_own.at[turn], dst_ref=dot_in.at[turn, shift - 1],
+            send_sem=dot_send.at[turn, shift - 1], recv_sem=dot_recv.at[turn, shift - 1],
+            device_id=(my_row, lax.rem(my_col + shift, 4)), device_id_type=MESH,
+        )
+
+    def pack(gamma, delta):
+        place_of = lax.broadcasted_iota(jnp.int32, (nrhs, width), 1)
+        gamma = jnp.sum(gamma, axis=1, keepdims=True)
+        delta = jnp.sum(delta, axis=1, keepdims=True)
+        return jnp.where(place_of == 0, gamma, jnp.where(place_of == 1, delta, 0.0))
+
+    def unpack(turn):
+        total = [dot_own[turn]] + [dot_in[turn, (3 - my_col_shift)] for my_col_shift in (1, 2, 3)]
+        total = (total[0] + total[2]) + (total[1] + total[3])
+        return total[:, 0:1], total[:, 1:2]
+
+    @pl.loop(0, steps)
+    def _(i):
+        fetch(i).wait()
+        parts = split(a_buf[i])
+        a_split[i] = parts
+        part[0, :, tile_lanes(i)] = fold(times_transposed(v_split[...], parts), nrhs, width)
+
+    pl.semaphore_wait(
+        barrier,
+        3 + (group - 1) + jnp.where(place > 0, 1, 0) + jnp.where(place < depth - 1, 1, 0),
+    )
+    finish_first = reduce_and_spread(0)
+
+    zeros = jnp.zeros((nrhs, width), jnp.float32)
+
+    def first_dots(t, carry):
+        lanes = tile_lanes(t)
+        u = u_buf[:, lanes]
+        return carry[0] + b_ref[:, lanes] * u, carry[1] + image[0, :, lanes] * u
+
+    dot_own[0] = pack(*lax.fori_loop(0, tiles, first_dots, (zeros, zeros)))
+    for shift in (2, 1, 3):
+        dots_copy(0, shift).start()
+
+    precondition(image.at[0], m_buf)
+
+    @pl.loop(0, steps)
+    def _(i):
+        part[1, :, tile_lanes(i)] = fold(times_transposed(v_split[...], a_split[i]), nrhs, width)
+
+    for shift in range(1, 4):
+        dots_copy(0, shift).wait()
+    finish_first()
+    finish_second = reduce_and_spread(1)
+
+    gamma0, delta0 = unpack(0)
+    alpha0 = gamma0 / delta0
+
+    def second_dots(t, carry):
+        lanes = tile_lanes(t)
+        res = b_ref[:, lanes] - alpha0 * image[0, :, lanes]
+        pre = u_buf[:, lanes] - alpha0 * m_buf[:, lanes]
+        img = image[0, :, lanes] - alpha0 * image[1, :, lanes]
+        res_ref[:, lanes] = res
+        m_buf[:, lanes] = pre
+        return carry[0] + res * pre, carry[1] + img * pre
+
+    dot_own[1] = pack(*lax.fori_loop(0, tiles, second_dots, (zeros, zeros)))
+    for shift in (2, 1, 3):
+        dots_copy(1, shift).start()
+    for shift in range(1, 4):
+        dots_copy(1, shift).wait()
+    gamma1, delta1 = unpack(1)
+    beta = gamma1 / gamma0
+    alpha1 = gamma1 / (delta1 - beta * gamma1 / alpha0)
+
+    @pl.loop(0, tiles)
+    def _(t):
+        lanes = tile_lanes(t)
+        u = u_buf[:, lanes]
+        w = image[0, :, lanes]
+        img = w - alpha0 * image[1, :, lanes]
+        sol_ref[:, lanes] = alpha0 * u + alpha1 * (m_buf[:, lanes] + beta * u)
+        res_ref[:, lanes] = res_ref[:, lanes] - alpha1 * (img + beta * w)
+
+    finish_second()
+
+
+def fused_body(row_count, group, normal_matrix, right_side, tile_inverse, order_ids):
+    block_rows, block_cols = normal_matrix.shape
+    nrhs = right_side.shape[1]
+    tiles, width = tile_inverse.shape[:2]
+    steps = block_rows // width
+    chunks = 3 if steps % 3 == 0 else 1
+    f32, bf16 = jnp.float32, jnp.bfloat16
+    out = jax.ShapeDtypeStruct((nrhs, block_cols), f32)
+    dma = pltpu.SemaphoreType.DMA
+    vmem = pl.BlockSpec(memory_space=pltpu.VMEM)
+    sol, res = pl.pallas_call(
+        functools.partial(kernel, row_count, group, chunks, width),
+        out_shape=(out, out),
+        in_specs=[pl.BlockSpec(memory_space=pl.ANY), vmem, vmem],
+        out_specs=(vmem, vmem),
+        scratch_shapes=[
+            pltpu.VMEM((steps, width, block_cols), f32),
+            pltpu.VMEM((steps, 2 * width, block_cols), bf16),
+            pltpu.VMEM((tiles, 2 * width, width), bf16),
+            pltpu.VMEM((2 * nrhs, block_cols), bf16),
+            pltpu.VMEM((nrhs, block_cols), f32),
+            pltpu.VMEM((nrhs, block_cols), f32),
+            pltpu.VMEM((2, nrhs, block_rows), f32),
+            pltpu.VMEM((2, nrhs // 2, block_rows), f32),
+            pltpu.VMEM((2, nrhs // 2, block_rows), f32),
+            pltpu.VMEM((2, nrhs // 2, block_rows), f32),
+            pltpu.VMEM((2, nrhs, block_rows), f32),
+            pltpu.VMEM((2, nrhs, block_cols), f32),
+            pltpu.VMEM((2, nrhs, width), f32),
+            pltpu.VMEM((2, 3, nrhs, width), f32),
+            dma((steps,)),
+            dma((2, 2)),
+            dma((2, 2)),
+            dma((2, 2)),
+            dma((2, chunks)),
+            dma((2, 2, chunks)),
+            dma((2, group - 1, chunks)),
+            dma((2, group - 1, chunks)),
+            dma((2, 3)),
+            dma((2, 3)),
+        ],
+        compiler_params=pltpu.CompilerParams(
+            collective_id=0, has_side_effects=True, vmem_limit_bytes=60 * 1024 * 1024
+        ),
+    )(normal_matrix, masked_tiles(tile_inverse, order_ids), right_side.T)
+    return sol.T, res.T
+
+
+def body(row_count, col_count, normal_matrix, right_side, tile_inverse, order_ids):
+    block_rows, block_cols = normal_matrix.shape
+    width = tile_inverse.shape[1]
+    group = block_cols // block_rows
+    fits = (
+        col_count == 4
+        and group > 1
+        and row_count == group * col_count
+        and block_rows % width == 0
+        and width % 128 == 0
+        and right_side.shape[1] % 32 == 0
+    )
+    if fits:
+        return fused_body(row_count, group, normal_matrix, right_side, tile_inverse, order_ids)
+    return plain_body(normal_matrix, right_side, tile_inverse, order_ids)
+
+
 def solution(mesh):
     return jax.shard_map(
-        body,
+        functools.partial(body, mesh.shape["row"], mesh.shape["col"]),
         mesh=mesh,
         in_specs=(P("row", "col"), P("col", None), P("col", None, None), P("col")),
         out_specs=(P("col", None), P("col", None)),

time: 251 us -> 79.5 us (0.32)
  waiting for transfers between devices: 190 us -> 0 us
  Pallas kernels: 0 us -> 73.4 us
  matrix products: 30 us -> 0 us
  between operations: 13.8 us -> 0.65 us
  blocking collectives: 11.5 us -> 0 us
    psum x2 -> x0, waiting for transfers between devices: 141 us -> none  [apply_matrix(): return lax.psum(partial_value, 'row')]
    pallas_call x0 -> x1, Pallas kernels: none -> 73.4 us  [fused_body(): pl.pallas_call(functools.partial(kernel, row_count, group, chunks, width)...]
    all_gather x2 -> x0, waiting for transfers between devices: 49.8 us -> none  [apply_matrix(): gathered = lax.all_gather(vector, 'col', axis=0, tiled=True)]
    dot_general x4 -> x0, matrix products: 30 us -> none  [the longest x2 22.7 us: apply_matrix(): lax.dot_general(normal_matrix, row_piece, (((0,), (0,)), ((), ())), preci...]
    psum x2 -> x0, blocking collectives: 11.5 us -> none  [body(): lax.psum((jnp.sum(residual * precond_res, axis=0), jnp.sum(image_res * pr...]
    unnamed x10 -> x4, local copies, waits for them, and re-layouts: 0.02 us -> 2.8 us
  transfers between devices with their start and end apart: 4 -> 0, of which waited for: 4 -> 0; matrix products, arithmetic and copies ran while one was open for 0% -> 0% of each run, Pallas kernels for 0% -> 0%
where the time goes in v1:
time: 79.5 us; the launch traced here: 79.3 us
  Pallas kernels  73.4 us (92%)
  local copies, waits for them, and re-layouts  2.8 us (4%)
  other arithmetic  2.38 us (3%)
    pallas_call x1, Pallas kernels, fused_body(): pl.pallas_call(functools.partial(kernel, row_count, group, chunks, width)...  73.4 us
    unnamed x4, local copies, waits for them, and re-layouts  2.8 us
    select_n x1, other arithmetic, masked_tiles(): return jnp.where(same_order, tile_inverse, jnp.float32(0.0))  2.38 us

profile of v1, /device:TPU:0, one launch (start us, length us, event | category | flops | bytes accessed | tf_op | source)
XLA Modules:
  0.0 79.3 jit_solution(8259638542407083551)
XLA Ops:
  0.6 2.4 %compare_select_fusion.tile_ref = f32[18,128,128]{2,1,0:T(8,128)} fusion(f32[18,128,128]{2,1,0:T(8,128)} %param.6, s32[18,128]{1,0:T(8,128)} %bitcast.7), kind=kLoop, calls=%fused_computation | loop fusion | flops 589824 | bytes 2368512 | tf_op jit(solution)/shard_map/jit(_where)/select_n | solution.py:19
  3.0 73.4 %shard_map.59 = (f32[64,2304]{1,0:T(8,128)}, f32[64,2304]{1,0:T(8,128)}) custom-call(f32[1152,2304]{1,0:T(8,128)} %a_ref.1, f32[18,128,128]{2,1,0:T(8,128)} %compare_select_fusion.tile_ref, f32[64,2304]{1,0:T(8,128)} %bitcast.4), custom_call_target="tpu_custom_call" | custom-call | tf_op jit(solution)/shard_map/pallas_call | solution.py:351
  76.5 0.0 copy-start
  76.5 2.0 %copy.8 = f32[2304,64]{0,1:T(8,128)} copy(f32[2304,64]{0,1:T(8,128)} %bitcast.6) | data formatting | bytes 1179648
  78.4 0.0 copy-done
  78.5 0.8 %copy.9 = f32[2304,64]{0,1:T(8,128)} copy(f32[2304,64]{0,1:T(8,128)S(1)} %bitcast.5) | data formatting | bytes 1179648
Async XLA Ops:
  76.5 2.0 %copy-start = (f32[64,2304]{1,0:T(8,128)S(1)}, f32[64,2304]{1,0:T(8,128)}, u32[]{:S(2)}) copy-start(f32[64,2304]{1,0:T(8,128)} %get-tuple-element.5) | copy-start | bytes 1769476

commit v2 on v1

--- a/solution.py
+++ b/solution.py
@@ -9,6 +9,8 @@
 
 ITERS = 2
 MESH = pl.DeviceIdType.MESH
+CHUNKS = 9
+LAGS = (0, 2, 6, 8)
 
 
 def masked_tiles(tile_inverse, order_ids):
@@ -100,11 +102,11 @@
 
 def kernel(
     row_count, group, chunks, width,
-    a_ref, tile_ref, b_ref,
+    a_ref, tile_ref, b_ref, ids_ref,
     sol_ref, res_ref,
     a_buf, a_split, tile_split, v_split, u_buf, m_buf,
     part, near, half, far, full, image,
-    dot_own, dot_in,
+    dot_own, dot_in, sums, i_buf, ids_buf,
     a_sem, near_sem, far_sem, full_sem, line_recv, line_send, side_recv, side_send, dot_send, dot_recv,
 ):
     my_row, my_col = lax.axis_index("row"), lax.axis_index("col")
@@ -148,80 +150,69 @@
     def tile_lanes(t):
         return pl.ds(pl.multiple_of(t * width, width), width)
 
-    def precondition(source, target):
-        @pl.loop(0, tiles)
-        def _(t):
-            lanes = tile_lanes(t)
-            value = fold(times_transposed(split(source[:, lanes]), tile_split[t]), nrhs, width)
-            target[:, lanes] = value
-            v_split[:, lanes] = split(value)
+    def precondition_tile(t, value, target):
+        lanes = tile_lanes(t)
+        value = fold(times_transposed(split(value), tile_split[t]), nrhs, width)
+        target[:, lanes] = value
+        v_split[:, lanes] = split(value)
+
+    ids_buf[...] = jnp.zeros_like(ids_buf)
+    ids_buf[0:tiles] = ids_ref[...].astype(jnp.float32)
+    ids_across = ids_buf[...].T
+    for t in range(tiles):
+        same = ids_across[:, t : t + 1] == ids_buf[t : t + 1]
+        tile_split[t] = split(jnp.where(same, tile_ref[t], 0.0))
 
     @pl.loop(0, tiles)
     def _(t):
-        tile_split[t] = split(tile_ref[t])
-
-    precondition(b_ref, u_buf)
-
-    def reduce_and_spread(turn):
-        def swap(source, target, sem, column):
+        precondition_tile(t, b_ref[:, tile_lanes(t)], u_buf)
+
+    mine = pl.ds(pl.multiple_of(core * hh, hh), hh)
+    other = pl.ds(pl.multiple_of((1 - core) * hh, hh), hh)
+    goes_up = jnp.logical_and(place >= my_col, place < depth - 1)
+    goes_down = jnp.logical_and(place <= my_col, place > 0)
+    per_chunk = steps // chunks
+
+    def multiply_and_spread(turn, make, use):
+        def swap(source, target, sem, column, q):
             return pltpu.make_async_remote_copy(
-                src_ref=source, dst_ref=target, send_sem=sem.at[turn, 0], recv_sem=sem.at[turn, 1],
+                src_ref=source, dst_ref=target, send_sem=sem.at[turn, 0, q], recv_sem=sem.at[turn, 1, q],
                 device_id=(my_row, column), device_id_type=MESH,
             )
 
-        mine = pl.ds(pl.multiple_of(core * hh, hh), hh)
-        other = pl.ds(pl.multiple_of((1 - core) * hh, hh), hh)
-        first = swap(part.at[turn, other], near.at[turn], near_sem, partner)
-        first.start()
-        first.wait()
-        half[turn] = part[turn, mine] + near[turn]
-        second = swap(half.at[turn], far.at[turn], far_sem, across)
-        second.start()
-        second.wait()
-        full[turn, mine] = half[turn] + far[turn]
-        third = swap(full.at[turn, mine], full.at[turn, mine], full_sem, partner)
-        third.start()
-        third.wait()
-
-        @pl.when(place == my_col)
-        def _():
-            start = pl.multiple_of(lane * block_rows, width)
-            image[turn, :, pl.ds(start, block_rows)] = full[turn]
+        def cut(q):
+            return pl.ds(q * piece, piece)
+
+        def first(q):
+            return swap(part.at[turn, other, cut(q)], near.at[turn, :, cut(q)], near_sem, partner, q)
+
+        def second(q):
+            return swap(half.at[turn, :, cut(q)], far.at[turn, :, cut(q)], far_sem, across, q)
+
+        def third(q):
+            return swap(full.at[turn, mine, cut(q)], full.at[turn, mine, cut(q)], full_sem, partner, q)
 
         def lanes_of(owner, q):
-            start = pl.multiple_of(owner * block_rows + q * piece, width)
-            return image.at[turn, :, pl.ds(start, piece)]
+            return pl.ds(pl.multiple_of(owner * block_rows + q * piece, width), piece)
 
         def along(q, way, target_row):
             return pltpu.make_async_remote_copy(
-                src_ref=lanes_of(lane, q), dst_ref=lanes_of(lane, q),
+                src_ref=image.at[turn, :, lanes_of(lane, q)], dst_ref=image.at[turn, :, lanes_of(lane, q)],
                 send_sem=line_send.at[turn, way, q], recv_sem=line_recv.at[turn, q],
                 device_id=(target_row, my_col), device_id_type=MESH,
             )
 
-        def sideways(q, shift):
-            side = place * group + lax.rem(lane + shift, group)
+        def sideways(q, shift, owner, side):
             return pltpu.make_async_remote_copy(
-                src_ref=lanes_of(lane, q), dst_ref=lanes_of(lane, q),
+                src_ref=image.at[turn, :, lanes_of(owner, q)], dst_ref=image.at[turn, :, lanes_of(owner, q)],
                 send_sem=side_send.at[turn, shift - 1, q], recv_sem=side_recv.at[turn, shift - 1, q],
                 device_id=(side, my_col), device_id_type=MESH,
             )
 
-        def arrived(q, shift):
-            origin = lax.rem(lane + group - shift, group)
-            return pltpu.make_async_remote_copy(
-                src_ref=lanes_of(origin, q), dst_ref=lanes_of(origin, q),
-                send_sem=side_send.at[turn, shift - 1, q], recv_sem=side_recv.at[turn, shift - 1, q],
-                device_id=(place * group + origin, my_col), device_id_type=MESH,
-            )
-
-        goes_up = jnp.logical_and(place >= my_col, place < depth - 1)
-        goes_down = jnp.logical_and(place <= my_col, place > 0)
-        for q in range(chunks):
-            @pl.when(place != my_col)
-            def _():
-                along(q, 0, my_row).wait_recv()
-
+        def outgoing(q, shift):
+            return sideways(q, shift, lane, place * group + lax.rem(lane + shift, group))
+
+        def pass_on(q):
             @pl.when(goes_up)
             def _():
                 along(q, 0, my_row + group).start()
@@ -231,11 +222,59 @@
                 along(q, 1, my_row - group).start()
 
             for shift in range(1, group):
-                sideways(q, shift).start()
-
+                outgoing(q, shift).start()
+
+        def stage0(q):
+            @pl.loop(q * per_chunk, (q + 1) * per_chunk)
+            def _(i):
+                part[turn, :, tile_lanes(i)] = make(i)
+
+            if turn == 0 and q == 0:
+                pl.semaphore_wait(
+                    barrier,
+                    3 + (group - 1) + jnp.where(place > 0, 1, 0) + jnp.where(place < depth - 1, 1, 0),
+                )
+            first(q).start()
+
+        def stage1(q):
+            first(q).wait()
+            half[turn, :, cut(q)] = part[turn, mine, cut(q)] + near[turn, :, cut(q)]
+            second(q).start()
+
+        def stage2(q):
+            second(q).wait()
+            full[turn, mine, cut(q)] = half[turn, :, cut(q)] + far[turn, :, cut(q)]
+            third(q).start()
+
+        def stage3(q):
+            third(q).wait()
+
+            @pl.when(place == my_col)
+            def _():
+                image[turn, :, lanes_of(lane, q)] = full[turn, :, cut(q)]
+                pass_on(q)
+
+        for tick in range(chunks + LAGS[-1]):
+            for lag, stage in zip(LAGS, (stage0, stage1, stage2, stage3)):
+                if 0 <= tick - lag < chunks:
+                    stage(tick - lag)
+
+        @pl.when(place != my_col)
+        def _():
+            for q in range(chunks):
+                along(q, 0, my_row).wait_recv()
+                pass_on(q)
+
+        if turn == 1:
+            for shift in range(1, 4):
+                dots_copy(0, shift).wait()
+        for q in range(chunks):
+            use(lane * steps + q * per_chunk, per_chunk)
         for q in range(chunks):
             for shift in range(1, group):
-                arrived(q, shift).wait_recv()
+                origin = lax.rem(lane + group - shift, group)
+                sideways(q, shift, origin, place * group + origin).wait_recv()
+                use(origin * steps + q * per_chunk, per_chunk)
 
         def finish():
             for q in range(chunks):
@@ -248,7 +287,7 @@
                     along(q, 1, my_row - group).wait_send()
 
                 for shift in range(1, group):
-                    sideways(q, shift).wait_send()
+                    outgoing(q, shift).wait_send()
 
         return finish
 
@@ -270,58 +309,60 @@
         total = (total[0] + total[2]) + (total[1] + total[3])
         return total[:, 0:1], total[:, 1:2]
 
-    @pl.loop(0, steps)
-    def _(i):
+    sums[...] = jnp.zeros_like(sums)
+
+    def first_product(i):
         fetch(i).wait()
         parts = split(a_buf[i])
         a_split[i] = parts
-        part[0, :, tile_lanes(i)] = fold(times_transposed(v_split[...], parts), nrhs, width)
-
-    pl.semaphore_wait(
-        barrier,
-        3 + (group - 1) + jnp.where(place > 0, 1, 0) + jnp.where(place < depth - 1, 1, 0),
-    )
-    finish_first = reduce_and_spread(0)
-
-    zeros = jnp.zeros((nrhs, width), jnp.float32)
-
-    def first_dots(t, carry):
-        lanes = tile_lanes(t)
-        u = u_buf[:, lanes]
-        return carry[0] + b_ref[:, lanes] * u, carry[1] + image[0, :, lanes] * u
-
-    dot_own[0] = pack(*lax.fori_loop(0, tiles, first_dots, (zeros, zeros)))
+        return fold(times_transposed(v_split[...], parts), nrhs, width)
+
+    def second_product(i):
+        return fold(times_transposed(v_split[...], a_split[i]), nrhs, width)
+
+    def first_use(begin, count):
+        @pl.loop(begin, begin + count)
+        def _(t):
+            lanes = tile_lanes(t)
+            u, w = u_buf[:, lanes], image[0, :, lanes]
+            sums[0] += b_ref[:, lanes] * u
+            sums[1] += w * u
+            precondition_tile(t, w, m_buf)
+
+    finish_first = multiply_and_spread(0, first_product, first_use)
+    dot_own[0] = pack(sums[0], sums[1])
     for shift in (2, 1, 3):
         dots_copy(0, shift).start()
-
-    precondition(image.at[0], m_buf)
-
-    @pl.loop(0, steps)
-    def _(i):
-        part[1, :, tile_lanes(i)] = fold(times_transposed(v_split[...], a_split[i]), nrhs, width)
-
+    sums[...] = jnp.zeros_like(sums)
+
+    def second_use(begin, count):
+        gamma0, delta0 = unpack(0)
+        alpha0 = gamma0 / delta0
+
+        @pl.loop(begin, begin + count)
+        def _(t):
+            lanes = tile_lanes(t)
+            w, u = image[0, :, lanes], u_buf[:, lanes]
+            res = b_ref[:, lanes] - alpha0 * w
+            pre = u - alpha0 * m_buf[:, lanes]
+            img = w - alpha0 * image[1, :, lanes]
+            res_ref[:, lanes] = res
+            sol_ref[:, lanes] = alpha0 * u
+            m_buf[:, lanes] = pre
+            i_buf[:, lanes] = img
+            sums[0] += res * pre
+            sums[1] += img * pre
+
+    finish_second = multiply_and_spread(1, second_product, second_use)
+    dot_own[1] = pack(sums[0], sums[1])
+    for shift in (2, 1, 3):
+        dots_copy(1, shift).start()
+    finish_first()
+    finish_second()
     for shift in range(1, 4):
-        dots_copy(0, shift).wait()
-    finish_first()
-    finish_second = reduce_and_spread(1)
-
+        dots_copy(1, shift).wait()
     gamma0, delta0 = unpack(0)
     alpha0 = gamma0 / delta0
-
-    def second_dots(t, carry):
-        lanes = tile_lanes(t)
-        res = b_ref[:, lanes] - alpha0 * image[0, :, lanes]
-        pre = u_buf[:, lanes] - alpha0 * m_buf[:, lanes]
-        img = image[0, :, lanes] - alpha0 * image[1, :, lanes]
-        res_ref[:, lanes] = res
-        m_buf[:, lanes] = pre
-        return carry[0] + res * pre, carry[1] + img * pre
-
-    dot_own[1] = pack(*lax.fori_loop(0, tiles, second_dots, (zeros, zeros)))
-    for shift in (2, 1, 3):
-        dots_copy(1, shift).start()
-    for shift in range(1, 4):
-        dots_copy(1, shift).wait()
     gamma1, delta1 = unpack(1)
     beta = gamma1 / gamma0
     alpha1 = gamma1 / (delta1 - beta * gamma1 / alpha0)
@@ -329,13 +370,8 @@
     @pl.loop(0, tiles)
     def _(t):
         lanes = tile_lanes(t)
-        u = u_buf[:, lanes]
-        w = image[0, :, lanes]
-        img = w - alpha0 * image[1, :, lanes]
-        sol_ref[:, lanes] = alpha0 * u + alpha1 * (m_buf[:, lanes] + beta * u)
-        res_ref[:, lanes] = res_ref[:, lanes] - alpha1 * (img + beta * w)
-
-    finish_second()
+        sol_ref[:, lanes] += alpha1 * (m_buf[:, lanes] + beta * u_buf[:, lanes])
+        res_ref[:, lanes] -= alpha1 * (i_buf[:, lanes] + beta * image[0, :, lanes])
 
 
 def fused_body(row_count, group, normal_matrix, right_side, tile_inverse, order_ids):
@@ -343,7 +379,7 @@
     nrhs = right_side.shape[1]
     tiles, width = tile_inverse.shape[:2]
     steps = block_rows // width
-    chunks = 3 if steps % 3 == 0 else 1
+    chunks = CHUNKS if steps % CHUNKS == 0 else 1
     f32, bf16 = jnp.float32, jnp.bfloat16
     out = jax.ShapeDtypeStruct((nrhs, block_cols), f32)
     dma = pltpu.SemaphoreType.DMA
@@ -351,7 +387,7 @@
     sol, res = pl.pallas_call(
         functools.partial(kernel, row_count, group, chunks, width),
         out_shape=(out, out),
-        in_specs=[pl.BlockSpec(memory_space=pl.ANY), vmem, vmem],
+        in_specs=[pl.BlockSpec(memory_space=pl.ANY), vmem, vmem, vmem],
         out_specs=(vmem, vmem),
         scratch_shapes=[
             pltpu.VMEM((steps, width, block_cols), f32),
@@ -368,10 +404,13 @@
             pltpu.VMEM((2, nrhs, block_cols), f32),
             pltpu.VMEM((2, nrhs, width), f32),
             pltpu.VMEM((2, 3, nrhs, width), f32),
+            pltpu.VMEM((2, nrhs, width), f32),
+            pltpu.VMEM((nrhs, block_cols), f32),
+            pltpu.VMEM((width, width), f32),
             dma((steps,)),
-            dma((2, 2)),
-            dma((2, 2)),
-            dma((2, 2)),
+            dma((2, 2, chunks)),
+            dma((2, 2, chunks)),
+            dma((2, 2, chunks)),
             dma((2, chunks)),
             dma((2, 2, chunks)),
             dma((2, group - 1, chunks)),
@@ -382,7 +421,7 @@
         compiler_params=pltpu.CompilerParams(
             collective_id=0, has_side_effects=True, vmem_limit_bytes=60 * 1024 * 1024
         ),
-    )(normal_matrix, masked_tiles(tile_inverse, order_ids), right_side.T)
+    )(normal_matrix, tile_inverse, right_side.T, order_ids.reshape(tiles, width))
     return sol.T, res.T
 
 
@@ -396,6 +435,7 @@
         and row_count == group * col_count
         and block_rows % width == 0
         and width % 128 == 0
+        and tile_inverse.shape[0] <= width
         and right_side.shape[1] % 32 == 0
     )
     if fits:

time: 79.5 us -> 63.8 us (0.80)
  Pallas kernels: 73.4 us -> 59.1 us
  other arithmetic: 2.38 us -> 0 us
  local copies, waits for them, and re-layouts: 2.8 us -> 3.83 us
    pallas_call x1, Pallas kernels: 73.4 us -> 59.1 us  [fused_body(): pl.pallas_call(functools.partial(kernel, row_count, group, chunks, width)...]
    select_n x1 -> x0, other arithmetic: 2.38 us -> none  [masked_tiles(): return jnp.where(same_order, tile_inverse, jnp.float32(0.0))]
    unnamed x4 -> x2, local copies, waits for them, and re-layouts: 2.8 us -> 3.83 us
where the time goes in v2:
time: 63.8 us; the launch traced here: 63.6 us
  Pallas kernels  59.1 us (93%)
  local copies, waits for them, and re-layouts  3.83 us (6%)
  between operations  0.64 us (1%)
    pallas_call x1, Pallas kernels, fused_body(): pl.pallas_call(functools.partial(kernel, row_count, group, chunks, width)...  59.1 us
    unnamed x2, local copies, waits for them, and re-layouts  3.83 us

profile of v2, /device:TPU:0, one launch (start us, length us, event | category | flops | bytes accessed | tf_op | source)
XLA Modules:
  0.0 63.6 jit_solution(13776741106202258781)
XLA Ops:
  0.6 59.1 %shard_map.59 = (f32[64,2304]{1,0:T(8,128)}, f32[64,2304]{1,0:T(8,128)}) custom-call(f32[1152,2304]{1,0:T(8,128)} %a_ref.1, f32[18,128,128]{2,1,0:T(8,128)} %tile_ref.1, f32[64,2304]{1,0:T(8,128)} %bitcast.4, s32[18,128]{1,0:T(8,128)} %bitcast.7), custom_call_target="tpu_custom_call" | custom-call | tf_op jit(solution)/shard_map/pallas_call | solution.py:387
  59.8 1.9 %copy.8 = f32[2304,64]{0,1:T(8,128)} copy(f32[2304,64]{0,1:T(8,128)} %bitcast.6) | data formatting | bytes 1179648
  61.7 1.9 %copy.9 = f32[2304,64]{0,1:T(8,128)} copy(f32[2304,64]{0,1:T(8,128)} %bitcast.5) | data formatting | bytes 1179648
